TPU v7x, 32 devices: a whole 2x2x4 slice. The times are simulated.
32 devices in a mesh: dp: 4 (over x, core), rows: 8 (over z, y).
Axes of the slice: x: 2, y: 2, z: 4, core: 2. Of those that a mesh axis runs over, the one named last changes fastest.
Arguments:
- grads: bfloat16 [2, 4096, 14336], P(None, 'rows', 'dp'), may hold values from -64 to 64
- basis: bfloat16 [2, 4096, 512], P(None, 'rows'), may hold values from -0.09375 to 0.09375
- moment1: float32 [2, 512, 14336], P(None, 'rows', 'dp'), may hold values from -0.3 to 0.3
- moment2: float32 [2, 512, 14336], P(None, 'rows', 'dp'), may hold values from 0.001 to 0.03
- weights: bfloat16 [2, 4096, 14336], P(None, 'rows', 'dp'), may hold values from -0.09375 to 0.09375
Outputs:
- new_weights: bfloat16 [2, 4096, 14336], P(None, 'rows')
- new_moment1: float32 [2, 512, 14336], P(None, 'rows', 'dp')
- new_moment2: float32 [2, 512, 14336], P(None, 'rows', 'dp')
All inputs are finite; a program needn't handle non-finite values.
Results may differ from a plain program's by a relative error of at most 0.00115.
The roundings to bfloat16 on the way count: a program that leaves them out, or rounds other values in their place, can miss the bound.
Values may be sent and summed in bfloat16 or wider, within the bound.
A program may use at most 128 MiB of HBM per device.

v0:
```python
import math
import jax
import jax.numpy as jnp
from jax import lax
from jax.sharding import PartitionSpec as P

D = 4096
FF = 14336
MATS = 2
STEP = 10


def moment_step(projected, moment1, moment2, total):
    limit = 1.0 * math.sqrt(MATS * D * FF)
    scale = limit / jnp.maximum(jnp.sqrt(total), limit)
    scaled = scale * projected
    first = 0.9 * moment1 + 0.1 * scaled
    second = 0.999 * moment2 + 0.001 * scaled * scaled
    first_bias_correction = 1.0 - 0.9**STEP
    second_fix = 1.0 - 0.999**STEP
    low_rank_update = (
        first / first_bias_correction / (jnp.sqrt(second / second_fix) + 1e-08)
    ).astype(jnp.bfloat16)
    return (first, second, low_rank_update)


def local(grads, basis, moment1, moment2, weights):
    grad_wide = grads.astype(jnp.float32)
    own_squares = jnp.sum(grad_wide * grad_wide)
    partial_norm_value = jnp.einsum(
        "yka,ykx->yax", basis, grads, preferred_element_type=jnp.float32
    )
    total = lax.psum(own_squares, ("dp", "rows"))
    projected = lax.psum_scatter(partial_norm_value, "rows", scatter_dimension=1, tiled=True)
    first, second, low_rank_update = moment_step(projected, moment1, moment2, total)
    projected_back = jnp.einsum(
        "auw,awl->aul",
        basis,
        lax.all_gather(low_rank_update, "rows", axis=1, tiled=True),
        preferred_element_type=jnp.float32,
    )
    fresh = (weights.astype(jnp.float32) - 0.5 * projected_back).astype(jnp.bfloat16)
    whole_rows = lax.all_gather(fresh, "dp", axis=2, tiled=True)
    return (whole_rows, first, second)


def solution(mesh):
    return jax.shard_map(
        local,
        mesh=mesh,
        in_specs=(
            P(None, "rows", "dp"),
            P(None, "rows", None),
            P(None, "rows", "dp"),
            P(None, "rows", "dp"),
            P(None, "rows", "dp"),
        ),
        out_specs=(P(None, "rows", None), P(None, "rows", "dp"), P(None, "rows", "dp")),
        check_vma=False,
    )
```

profile of v0, /device:TPU:0, one launch (start us, length us, event | category | flops | bytes accessed | tf_op | source)
XLA Modules:
  0.0 606.6 jit_solution(13229460266157329375)
XLA Ops:
  7.2 0.0 copy-start
  7.2 0.0 reduce-scatter.2.cloned.1.call-start
  7.2 1.2 copy-done
  8.4 10.7 %fusion.3 = f32[2,512,3584]{2,1,0:T(8,128)} fusion(bf16[2,512,512]{2,1,0:T(8,128)(2,1)S(1)} %copy-done, bf16[2,512,3584]{2,1,0:T(8,128)(2,1)} %param.5), kind=kOutput, calls=%fused_computation.7 | convolution fusion | flops 3758096384 | bytes 23068672 | tf_op jit(solution)/shard_map/yka,ykx->yax/dot_general | solution.py:30
  19.1 0.0 reduce-scatter.2.cloned.1.call-update
  19.1 0.0 copy-start.2
  19.1 0.0 all-gather.3.cloned.1.call-start
  19.1 7.6 %multiply_reduce_fusion = f32[]{:T(128)} fusion(bf16[2,512,3584]{2,1,0:T(8,128)(2,1)} %param.5), kind=kLoop, calls=%fused_computation.2 | loop fusion | flops 11010047 | bytes 7340036 | tf_op jit(solution)/shard_map/reduce_sum | solution.py:29
  26.7 47.2 %psum.7 = f32[]{:T(128)} all-reduce(f32[]{:T(128)} %multiply_reduce_fusion), channel_id=1, replica_groups=mesh['dp'=4,'rows'=8] {'dp','rows'}, use_global_device_ids=true, to_apply=%region_1.0 | all-reduce | flops 1 | bytes 8 | tf_op jit(solution)/shard_map/psum | solution.py:33
  74.6 185.0 %reduce-scatter.2.cloned.1.call-done = f32[2,64,3584]{2,1,0:T(8,128)} async-done(((f32[2,512,3584]{2,1,0:T(8,128)}), f32[2,64,3584]{2,1,0:T(8,128)}) %reduce-scatter.2.cloned.1.call-update) | async-done | bytes 1835024 | tf_op jit(solution)/shard_map/reduce_scatter | solution.py:34
  259.6 0.0 copy-done.2
  259.6 4.9 divide_convert_fusion
  264.5 0.0 all-gather.3.cloned.1.call-update
  264.6 0.0 all-gather.5.cloned.1.call-start
  264.6 10.1 %copy.8 = bf16[2,512,3584]{1,2,0:T(8,128)(2,1)} copy(bf16[2,512,3584]{2,1,0:T(8,128)(2,1)} %param.9) | data formatting | bytes 14680064 | tf_op args[4]
  274.7 100.6 %all-gather.3.cloned.1.call-done = bf16[2,512,3584]{2,1,0:T(8,128)(2,1)} async-done(((bf16[2,64,3584]{2,1,0:T(8,128)(2,1)}), bf16[2,512,3584]{2,1,0:T(8,128)(2,1)}) %all-gather.3.cloned.1.call-update) | async-done | bytes 7340048 | tf_op jit(solution)/shard_map/all_gather | solution.py:39
  375.3 12.5 %fusion = bf16[2,512,3584]{1,2,0:T(8,128)(2,1)} fusion(bf16[2,512,3584]{1,2,0:T(8,128)(2,1)} %copy.8, bf16[2,512,3584]{2,1,0:T(8,128)(2,1)} %all-gather.3.cloned.1.call-done, bf16[2,512,512]{2,1,0:T(8,128)(2,1)S(1)} %copy-done), kind=kOutput, calls=%fused_computation.1 | convolution fusion | flops 3772776448 | bytes 23068672 | tf_op jit(solution)/shard_map/auw,awl->aul/dot_general | solution.py:36
  387.8 0.0 all-gather.5.cloned.1.call-update
  387.8 176.0 %all-gather.5.cloned.1.call-done = bf16[2,512,14336]{1,2,0:T(8,128)(2,1)} async-done(((bf16[2,512,3584]{1,2,0:T(8,128)(2,1)}), bf16[2,512,14336]{1,2,0:T(8,128)(2,1)}) %all-gather.5.cloned.1.call-update) | async-done | bytes 29360144 | tf_op jit(solution)/shard_map/all_gather | solution.py:43
  563.8 0.0 copy-start.1
  563.8 36.3 %copy.10 = bf16[2,512,14336]{2,1,0:T(8,128)(2,1)} copy(bf16[2,512,14336]{1,2,0:T(8,128)(2,1)} %all-gather.5.cloned.1.call-done) | data formatting | bytes 58720256
  600.0 0.0 copy-done.1
Async XLA Ops:
  7.2 1.2 copy-start
  7.2 252.4 %reduce-scatter.2.cloned.1.call-start = ((), (), s32[]{:S(2)}) async-start(), calls=%async_computation.1 | async-start | bytes 16515072 | tf_op jit(solution)/shard_map/reduce_scatter | solution.py:34
  19.1 240.5 %copy-start.2 = (f32[2,64,3584]{2,1,0:T(8,128)S(1)}, f32[2,64,3584]{2,1,0:T(8,128)}, u32[]{:S(2)}) copy-start(f32[2,64,3584]{2,1,0:T(8,128)} %param.7) | copy-start | bytes 5505028
  19.1 356.2 %all-gather.3.cloned.1.call-start = ((), (), s32[]{:S(2)}) async-start(), calls=%async_computation.2 | async-start | bytes 8257536 | tf_op jit(solution)/shard_map/all_gather | solution.py:39
  264.6 299.2 %all-gather.5.cloned.1.call-start = ((), (), s32[]{:S(2)}) async-start(), calls=%async_computation.3 | async-start | bytes 36700160 | tf_op jit(solution)/shard_map/all_gather | solution.py:43
  563.8 36.3 %copy-start.1 = (bf16[2,512,512]{2,1,0:T(8,128)(2,1)S(1)}, bf16[2,512,512]{2,1,0:T(8,128)(2,1)}, u32[]{:S(2)}) copy-start(bf16[2,512,512]{2,1,0:T(8,128)(2,1)} %param.6) | copy-start | bytes 3145732
Sparse Core Ops, SparseCore 0:
  19.2 240.3 reduce-scatter.1
  264.7 110.5 all-gather.2
  387.9 175.8 all-gather.4
where the time goes:
time: 608 us; the launch traced here: 607 us
  waiting for transfers between devices  462 us (76%)
  local copies, waits for them, and re-layouts  47.6 us (8%)
  blocking collectives  47.2 us (8%)
  matrix products  23.1 us (4%)
  between operations  14.5 us (2%)
  other arithmetic  12.5 us (2%)
    reduce_scatter x1, waiting for transfers between devices, local(): lax.psum_scatter(partial_norm_value, 'rows', scatter_dimension=1, tiled=T...  185 us
    all_gather x1, waiting for transfers between devices, local(): whole_rows = lax.all_gather(fresh, 'dp', axis=2, tiled=True)  176 us
    all_gather x1, waiting for transfers between devices, local(): lax.all_gather(low_rank_update, 'rows', axis=1, tiled=True)  101 us
    unnamed x8, local copies, waits for them, and re-layouts  47.6 us
    psum x1, blocking collectives, local(): total = lax.psum(own_squares, ('dp', 'rows'))  47.2 us
    dot_general x1, matrix products, local(): jnp.einsum('auw,awl->aul', basis, lax.all_gather(low_rank_update, 'rows',...  12.5 us
  transfers between devices with their start and end apart: 3, of which 3 were waited for; matrix products, arithmetic and copies ran while one was open for 3% of the time, Pallas kernels for 0%

commit v1 on v0

--- a/solution.py
+++ b/solution.py
@@ -36,7 +36,7 @@
     projected_back = jnp.einsum(
         "auw,awl->aul",
         basis,
-        lax.all_gather(low_rank_update, "rows", axis=1, tiled=True),
+        jnp.concatenate(lax.all_gather(low_rank_update, "rows"), axis=1),
         preferred_element_type=jnp.float32,
     )
     fresh = (weights.astype(jnp.float32) - 0.5 * projected_back).astype(jnp.bfloat16)

time: 608 us -> 615 us (1.012)
  local copies, waits for them, and re-layouts: 47.6 us -> 54.3 us
    reshape x0 -> x1, local copies, waits for them, and re-layouts: none -> 6.75 us  [local(): jnp.concatenate(lax.all_gather(low_rank_update, 'rows'), axis=1)]
where the time goes in v1:
time: 615 us; the launch traced here: 613 us
  waiting for transfers between devices  462 us (75%)
  local copies, waits for them, and re-layouts  54.3 us (9%)
  blocking collectives  47.2 us (8%)
  matrix products  23.1 us (4%)
  between operations  14.5 us (2%)
  other arithmetic  12.5 us (2%)
    reduce_scatter x1, waiting for transfers between devices, local(): lax.psum_scatter(partial_norm_value, 'rows', scatter_dimension=1, tiled=T...  185 us
    all_gather x1, waiting for transfers between devices, local(): whole_rows = lax.all_gather(fresh, 'dp', axis=2, tiled=True)  176 us
    all_gather x1, waiting for transfers between devices, local(): lax.all_gather(low_rank_update, 'rows')  101 us
    unnamed x8, local copies, waits for them, and re-layouts  47.6 us
    psum x1, blocking collectives, local(): total = lax.psum(own_squares, ('dp', 'rows'))  47.2 us
    dot_general x1, matrix products, local(): jnp.einsum('auw,awl->aul', basis, jnp.concatenate(lax.all_gather(low_rank...  12.5 us
  transfers between devices with their start and end apart: 3, of which 3 were waited for; matrix products, arithmetic and copies ran while one was open for 3% of the time, Pallas kernels for 0%

profile of v1, /device:TPU:0, one launch (start us, length us, event | category | flops | bytes accessed | tf_op | source)
XLA Modules:
  0.0 613.3 jit_solution(9775990279535990709)
XLA Ops:
  7.2 0.0 copy-start
  7.2 0.0 reduce-scatter.2.cloned.1.call-start
  7.2 1.2 copy-done
  8.4 10.7 %fusion.3 = f32[2,512,3584]{2,1,0:T(8,128)} fusion(bf16[2,512,512]{2,1,0:T(8,128)(2,1)S(1)} %copy-done, bf16[2,512,3584]{2,1,0:T(8,128)(2,1)} %param.5), kind=kOutput, calls=%fused_computation.7 | convolution fusion | flops 3758096384 | bytes 23068672 | tf_op jit(solution)/shard_map/yka,ykx->yax/dot_general | solution.py:30
  19.1 0.0 reduce-scatter.2.cloned.1.call-update
  19.1 0.0 copy-start.2
  19.1 0.0 all-gather.6.cloned.1.call-start
  19.1 7.6 %multiply_reduce_fusion = f32[]{:T(128)} fusion(bf16[2,512,3584]{2,1,0:T(8,128)(2,1)} %param.5), kind=kLoop, calls=%fused_computation.2 | loop fusion | flops 11010047 | bytes 7340036 | tf_op jit(solution)/shard_map/reduce_sum | solution.py:29
  26.7 47.2 %psum.7 = f32[]{:T(128)} all-reduce(f32[]{:T(128)} %multiply_reduce_fusion), channel_id=1, replica_groups=mesh['dp'=4,'rows'=8] {'dp','rows'}, use_global_device_ids=true, to_apply=%region_1.0 | all-reduce | flops 1 | bytes 8 | tf_op jit(solution)/shard_map/psum | solution.py:33
  74.6 185.0 %reduce-scatter.2.cloned.1.call-done = f32[2,64,3584]{2,1,0:T(8,128)} async-done(((f32[2,512,3584]{2,1,0:T(8,128)}), f32[2,64,3584]{2,1,0:T(8,128)}) %reduce-scatter.2.cloned.1.call-update) | async-done | bytes 1835024 | tf_op jit(solution)/shard_map/reduce_scatter | solution.py:34
  259.6 0.0 copy-done.2
  259.6 4.9 divide_convert_fusion
  264.5 0.0 all-gather.6.cloned.1.call-update
  264.6 0.0 all-gather.4.cloned.1.call-start
  264.6 10.1 %copy.21 = bf16[2,512,3584]{1,2,0:T(8,128)(2,1)} copy(bf16[2,512,3584]{2,1,0:T(8,128)(2,1)} %param.9) | data formatting | bytes 14680064 | tf_op args[4]
  274.7 100.6 %all-gather.6.cloned.1.call-done = bf16[16,64,3584]{2,1,0:T(8,128)(2,1)} async-done(((bf16[2,64,3584]{2,1,0:T(8,128)(2,1)}), bf16[16,64,3584]{2,1,0:T(8,128)(2,1)}) %all-gather.6.cloned.1.call-update) | async-done | bytes 7340048 | tf_op jit(solution)/shard_map/all_gather | solution.py:39
  375.3 6.7 %copy.23 = bf16[2,8,64,3584]{3,2,1,0:T(8,128)(2,1)} copy(bf16[2,8,64,3584]{3,2,0,1:T(8,128)(2,1)} %bitcast.12) | data formatting | bytes 14680064 | tf_op jit(solution)/shard_map/reshape | solution.py:39
  382.1 12.5 %fusion = bf16[2,512,3584]{1,2,0:T(8,128)(2,1)} fusion(bf16[2,512,3584]{1,2,0:T(8,128)(2,1)} %copy.21, bf16[2,512,3584]{2,1,0:T(8,128)(2,1)} %bitcast.13, bf16[2,512,512]{2,1,0:T(8,128)(2,1)S(1)} %copy-done), kind=kOutput, calls=%fused_computation.1 | convolution fusion | flops 3772776448 | bytes 23068672 | tf_op jit(solution)/shard_map/auw,awl->aul/dot_general | solution.py:36
  394.5 0.0 all-gather.4.cloned.1.call-update
  394.5 176.0 %all-gather.4.cloned.1.call-done = bf16[2,512,14336]{1,2,0:T(8,128)(2,1)} async-done(((bf16[2,512,3584]{1,2,0:T(8,128)(2,1)}), bf16[2,512,14336]{1,2,0:T(8,128)(2,1)}) %all-gather.4.cloned.1.call-update) | async-done | bytes 29360144 | tf_op jit(solution)/shard_map/all_gather | solution.py:43
  570.5 0.0 copy-start.1
  570.5 36.3 %copy.25 = bf16[2,512,14336]{2,1,0:T(8,128)(2,1)} copy(bf16[2,512,14336]{1,2,0:T(8,128)(2,1)} %all-gather.4.cloned.1.call-done) | data formatting | bytes 58720256
  606.8 0.0 copy-done.1
Async XLA Ops:
  7.2 1.2 copy-start
  7.2 252.4 %reduce-scatter.2.cloned.1.call-start = ((), (), s32[]{:S(2)}) async-start(), calls=%async_computation.1 | async-start | bytes 16515072 | tf_op jit(solution)/shard_map/reduce_scatter | solution.py:34
  19.1 240.5 %copy-start.2 = (f32[2,64,3584]{2,1,0:T(8,128)S(1)}, f32[2,64,3584]{2,1,0:T(8,128)}, u32[]{:S(2)}) copy-start(f32[2,64,3584]{2,1,0:T(8,128)} %param.7) | copy-start | bytes 5505028
  19.1 356.2 %all-gather.6.cloned.1.call-start = ((), (), s32[]{:S(2)}) async-start(), calls=%async_computation.3 | async-start | bytes 8257536 | tf_op jit(solution)/shard_map/all_gather | solution.py:39
  264.6 306.0 %all-gather.4.cloned.1.call-start = ((), (), s32[]{:S(2)}) async-start(), calls=%async_computation.2 | async-start | bytes 36700160 | tf_op jit(solution)/shard_map/all_gather | solution.py:43
  570.5 36.3 %copy-start.1 = (bf16[2,512,512]{2,1,0:T(8,128)(2,1)S(1)}, bf16[2,512,512]{2,1,0:T(8,128)(2,1)}, u32[]{:S(2)}) copy-start(bf16[2,512,512]{2,1,0:T(8,128)(2,1)} %param.6) | copy-start | bytes 3145732
Sparse Core Ops, SparseCore 0:
  19.2 240.3 reduce-scatter.1
  264.7 110.5 all-gather.5
  394.7 175.8 all-gather.3
